TPU v7x, 32 devices: a whole 2x2x4 slice. The times are simulated.
32 devices in a mesh: gx: 2 (over core), gy: 4 (over y, x), gz: 4 (over z).
Axes of the slice: x: 2, y: 2, z: 4, core: 2. Of those that a mesh axis runs over, the one named last changes fastest.
Arguments:
- queries: bfloat16 [128, 32, 128], P(None, 'gy'), may hold values from -6 to 6
- passages: bfloat16 [1024, 256, 128], P('gx', 'gz'), may hold values from -0.5 to 0.5
- passage_len: int32 [1024], P('gx'), may hold values from 32 to 256
- query_len: int32 [128], replicated, may hold values from 8 to 32
Outputs:
- log_probs: float32 [128, 1024], P(None, ('gx', 'gz'))
All inputs are finite; a program needn't handle non-finite values.
Results may differ from a plain program's by a relative error of at most 0.0003.
Values sent between devices are 32-bit elements; how exact they have to be, the bound alone decides.
A program may use at most 64 MiB of HBM per device.

v0:
```python
import math

import jax
import jax.numpy as jnp
from jax import lax
from jax.sharding import PartitionSpec as P

masked_low = -1e30


def combined_all(array, axis, combine):
    everything = jax.tree.map(lambda part: lax.all_gather(part, axis), array)
    initial = jax.tree.map(lambda part: part[0], everything)

    def turn(k, so_far):
        return combine(so_far, jax.tree.map(lambda part: part[k], everything))

    return lax.fori_loop(1, lax.axis_size(axis), turn, initial)


def token_maxima(queries, passages, passage_len):
    query_count = queries.shape[0]
    query_rows = queries.shape[1]
    width = queries.shape[2]
    passage_count = passages.shape[0]
    token_count = passages.shape[1]
    flat_queries = queries.reshape(query_count * query_rows, width)
    per_block = math.gcd(passage_count, 32)
    num_blocks = passage_count // per_block
    token_ids = lax.axis_index("gz") * token_count + jnp.arange(token_count, dtype=jnp.int32)
    tile_stack = passages.reshape(num_blocks, per_block * token_count, width)
    length_stack = passage_len.reshape(num_blocks, per_block)

    def block_maxima(packed):
        passage_tile, tile_len = packed
        scores = lax.dot_general(
            flat_queries, passage_tile, (((1,), (1,)), ((), ())), preferred_element_type=jnp.float32
        )
        scores = scores.reshape(query_count * query_rows, per_block, token_count)
        usable = token_ids[None, :] < tile_len[:, None]
        scores = jnp.where(usable[None], scores, masked_low)
        return jnp.max(scores, axis=2)

    pieces = lax.map(block_maxima, (tile_stack, length_stack))
    return jnp.transpose(pieces, (1, 0, 2)).reshape(query_count, query_rows, passage_count)


def join_pairs(earlier, other_pair):
    highest = jnp.maximum(earlier[0], other_pair[0])
    summed = earlier[1] * jnp.exp(earlier[0] - highest) + other_pair[1] * jnp.exp(
        other_pair[0] - highest
    )
    return (highest, summed)


def fold_peers(received):
    return jnp.max(received, axis=2)


def shards(queries, passages, passage_len, query_len):
    maxima = token_maxima(queries, passages, passage_len)
    query_count = maxima.shape[0]
    query_rows = maxima.shape[1]
    passage_count = maxima.shape[2]
    query_ids = lax.axis_index("gy") * query_rows + jnp.arange(query_rows, dtype=jnp.int32)
    counted = (query_ids[None, :] < query_len[:, None])[:, :, None]
    spread = maxima.reshape(query_count, query_rows, 1, passage_count)
    merged = fold_peers(lax.all_to_all(spread, "gz", split_axis=3, concat_axis=2, tiled=True))
    partial_value = jnp.sum(jnp.where(counted, merged, 0.0), axis=1)
    scores_here = lax.psum(partial_value, "gy")
    local_top = jnp.max(scores_here, axis=1)
    local_sum = jnp.sum(jnp.exp(scores_here - local_top[:, None]), axis=1)
    highest, summed = combined_all((local_top, local_sum), ("gx", "gz"), join_pairs)
    return scores_here - (highest + jnp.log(summed))[:, None]


def solution(mesh):
    return jax.shard_map(
        shards,
        mesh=mesh,
        in_specs=(P(None, "gy", None), P("gx", "gz", None), P("gx"), P()),
        out_specs=P(None, ("gx", "gz")),
        check_vma=False,
    )
```

profile of v0, /device:TPU:0, one launch (start us, length us, event | category | flops | bytes accessed | tf_op | source)
XLA Modules:
  0.0 207.8 jit_solution(13668500045373860605)
XLA Ops:
  7.3 40.6 %while.29 = (s32[]{:T(128)}, f32[16,1024,32]{1,2,0:T(8,128)S(1)}, s32[16,32]{1,0:T(8,128)S(1)}, bf16[16,2048,128]{2,1,0:T(8,128)(2,1)}, bf16[1024,128]{1,0:T(8,128)(2,1)}, /*index=5*/s32[]{:T(128)}, s32[]{:T(128)}) while((s32[]{:T(128)}, f32[16,1024,32]{1,2,0:T(8,128)S(1)}, s32[16,32]{1,0:T(8,128)S(1)}, ...), condition=%wide.region_2.3_spmd.clone, body=%wide.region_0.2_spmd.clone.sunk | while | flops 541034560 | bytes 1185241 | solution.py:44
  7.4 2.4 %select_reduce_fusion.3 = f32[1024,32]{0,1:T(8,128)S(1)} fusion(pred[32,64]{1,0:T(8,128)(4,1)S(1)} %broadcast_compare_fusion.3, bf16[1024,128]{1,0:T(8,128)(2,1)} %get-tuple-element.302, bf16[16,2048,128]{2,1,0:T(8,128)(2,1)} %get-tuple-element.301, s32[]{:T(128)} %get-tuple-element.291), kind=kOutput, calls=%fused_computation.7.clone.1 | convolution fusion | flops 541032448 | bytes 920064 | tf_op jit(solution)/shard_map/while/body/eval_jaxpr/dot_general | solution.py:36
  9.9 2.4 %select_reduce_fusion.3 = f32[1024,32]{0,1:T(8,128)S(1)} fusion(pred[32,64]{1,0:T(8,128)(4,1)S(1)} %broadcast_compare_fusion.3, bf16[1024,128]{1,0:T(8,128)(2,1)} %get-tuple-element.302, bf16[16,2048,128]{2,1,0:T(8,128)(2,1)} %get-tuple-element.301, s32[]{:T(128)} %get-tuple-element.291), kind=kOutput, calls=%fused_computation.7.clone.1 | convolution fusion | flops 541032448 | bytes 920064 | tf_op jit(solution)/shard_map/while/body/eval_jaxpr/dot_general | solution.py:36
  12.5 2.4 %select_reduce_fusion.3 = f32[1024,32]{0,1:T(8,128)S(1)} fusion(pred[32,64]{1,0:T(8,128)(4,1)S(1)} %broadcast_compare_fusion.3, bf16[1024,128]{1,0:T(8,128)(2,1)} %get-tuple-element.302, bf16[16,2048,128]{2,1,0:T(8,128)(2,1)} %get-tuple-element.301, s32[]{:T(128)} %get-tuple-element.291), kind=kOutput, calls=%fused_computation.7.clone.1 | convolution fusion | flops 541032448 | bytes 920064 | tf_op jit(solution)/shard_map/while/body/eval_jaxpr/dot_general | solution.py:36
  15.0 2.4 %select_reduce_fusion.3 = f32[1024,32]{0,1:T(8,128)S(1)} fusion(pred[32,64]{1,0:T(8,128)(4,1)S(1)} %broadcast_compare_fusion.3, bf16[1024,128]{1,0:T(8,128)(2,1)} %get-tuple-element.302, bf16[16,2048,128]{2,1,0:T(8,128)(2,1)} %get-tuple-element.301, s32[]{:T(128)} %get-tuple-element.291), kind=kOutput, calls=%fused_computation.7.clone.1 | convolution fusion | flops 541032448 | bytes 920064 | tf_op jit(solution)/shard_map/while/body/eval_jaxpr/dot_general | solution.py:36
  17.5 2.4 %select_reduce_fusion.3 = f32[1024,32]{0,1:T(8,128)S(1)} fusion(pred[32,64]{1,0:T(8,128)(4,1)S(1)} %broadcast_compare_fusion.3, bf16[1024,128]{1,0:T(8,128)(2,1)} %get-tuple-element.302, bf16[16,2048,128]{2,1,0:T(8,128)(2,1)} %get-tuple-element.301, s32[]{:T(128)} %get-tuple-element.291), kind=kOutput, calls=%fused_computation.7.clone.1 | convolution fusion | flops 541032448 | bytes 920064 | tf_op jit(solution)/shard_map/while/body/eval_jaxpr/dot_general | solution.py:36
  20.1 2.4 %select_reduce_fusion.3 = f32[1024,32]{0,1:T(8,128)S(1)} fusion(pred[32,64]{1,0:T(8,128)(4,1)S(1)} %broadcast_compare_fusion.3, bf16[1024,128]{1,0:T(8,128)(2,1)} %get-tuple-element.302, bf16[16,2048,128]{2,1,0:T(8,128)(2,1)} %get-tuple-element.301, s32[]{:T(128)} %get-tuple-element.291), kind=kOutput, calls=%fused_computation.7.clone.1 | convolution fusion | flops 541032448 | bytes 920064 | tf_op jit(solution)/shard_map/while/body/eval_jaxpr/dot_general | solution.py:36
  25.2 2.4 %select_reduce_fusion.3 = f32[1024,32]{0,1:T(8,128)S(1)} fusion(pred[32,64]{1,0:T(8,128)(4,1)S(1)} %broadcast_compare_fusion.3, bf16[1024,128]{1,0:T(8,128)(2,1)} %get-tuple-element.302, bf16[16,2048,128]{2,1,0:T(8,128)(2,1)} %get-tuple-element.301, s32[]{:T(128)} %get-tuple-element.291), kind=kOutput, calls=%fused_computation.7.clone.1 | convolution fusion | flops 541032448 | bytes 920064 | tf_op jit(solution)/shard_map/while/body/eval_jaxpr/dot_general | solution.py:36
  27.7 2.4 %select_reduce_fusion.3 = f32[1024,32]{0,1:T(8,128)S(1)} fusion(pred[32,64]{1,0:T(8,128)(4,1)S(1)} %broadcast_compare_fusion.3, bf16[1024,128]{1,0:T(8,128)(2,1)} %get-tuple-element.302, bf16[16,2048,128]{2,1,0:T(8,128)(2,1)} %get-tuple-element.301, s32[]{:T(128)} %get-tuple-element.291), kind=kOutput, calls=%fused_computation.7.clone.1 | convolution fusion | flops 541032448 | bytes 920064 | tf_op jit(solution)/shard_map/while/body/eval_jaxpr/dot_general | solution.py:36
  30.2 2.4 %select_reduce_fusion.3 = f32[1024,32]{0,1:T(8,128)S(1)} fusion(pred[32,64]{1,0:T(8,128)(4,1)S(1)} %broadcast_compare_fusion.3, bf16[1024,128]{1,0:T(8,128)(2,1)} %get-tuple-element.302, bf16[16,2048,128]{2,1,0:T(8,128)(2,1)} %get-tuple-element.301, s32[]{:T(128)} %get-tuple-element.291), kind=kOutput, calls=%fused_computation.7.clone.1 | convolution fusion | flops 541032448 | bytes 920064 | tf_op jit(solution)/shard_map/while/body/eval_jaxpr/dot_general | solution.py:36
  32.8 2.4 %select_reduce_fusion.3 = f32[1024,32]{0,1:T(8,128)S(1)} fusion(pred[32,64]{1,0:T(8,128)(4,1)S(1)} %broadcast_compare_fusion.3, bf16[1024,128]{1,0:T(8,128)(2,1)} %get-tuple-element.302, bf16[16,2048,128]{2,1,0:T(8,128)(2,1)} %get-tuple-element.301, s32[]{:T(128)} %get-tuple-element.291), kind=kOutput, calls=%fused_computation.7.clone.1 | convolution fusion | flops 541032448 | bytes 920064 | tf_op jit(solution)/shard_map/while/body/eval_jaxpr/dot_general | solution.py:36
  35.3 2.4 %select_reduce_fusion.3 = f32[1024,32]{0,1:T(8,128)S(1)} fusion(pred[32,64]{1,0:T(8,128)(4,1)S(1)} %broadcast_compare_fusion.3, bf16[1024,128]{1,0:T(8,128)(2,1)} %get-tuple-element.302, bf16[16,2048,128]{2,1,0:T(8,128)(2,1)} %get-tuple-element.301, s32[]{:T(128)} %get-tuple-element.291), kind=kOutput, calls=%fused_computation.7.clone.1 | convolution fusion | flops 541032448 | bytes 920064 | tf_op jit(solution)/shard_map/while/body/eval_jaxpr/dot_general | solution.py:36
  37.8 2.4 %select_reduce_fusion.3 = f32[1024,32]{0,1:T(8,128)S(1)} fusion(pred[32,64]{1,0:T(8,128)(4,1)S(1)} %broadcast_compare_fusion.3, bf16[1024,128]{1,0:T(8,128)(2,1)} %get-tuple-element.302, bf16[16,2048,128]{2,1,0:T(8,128)(2,1)} %get-tuple-element.301, s32[]{:T(128)} %get-tuple-element.291), kind=kOutput, calls=%fused_computation.7.clone.1 | convolution fusion | flops 541032448 | bytes 920064 | tf_op jit(solution)/shard_map/while/body/eval_jaxpr/dot_general | solution.py:36
  40.4 2.4 %select_reduce_fusion.3 = f32[1024,32]{0,1:T(8,128)S(1)} fusion(pred[32,64]{1,0:T(8,128)(4,1)S(1)} %broadcast_compare_fusion.3, bf16[1024,128]{1,0:T(8,128)(2,1)} %get-tuple-element.302, bf16[16,2048,128]{2,1,0:T(8,128)(2,1)} %get-tuple-element.301, s32[]{:T(128)} %get-tuple-element.291), kind=kOutput, calls=%fused_computation.7.clone.1 | convolution fusion | flops 541032448 | bytes 920064 | tf_op jit(solution)/shard_map/while/body/eval_jaxpr/dot_general | solution.py:36
  45.5 2.4 %select_reduce_fusion.3 = f32[1024,32]{0,1:T(8,128)S(1)} fusion(pred[32,64]{1,0:T(8,128)(4,1)S(1)} %broadcast_compare_fusion.3, bf16[1024,128]{1,0:T(8,128)(2,1)} %get-tuple-element.302, bf16[16,2048,128]{2,1,0:T(8,128)(2,1)} %get-tuple-element.301, s32[]{:T(128)} %get-tuple-element.291), kind=kOutput, calls=%fused_computation.7.clone.1 | convolution fusion | flops 541032448 | bytes 920064 | tf_op jit(solution)/shard_map/while/body/eval_jaxpr/dot_general | solution.py:36
  47.9 6.2 %copy.11 = f32[1024,16,32]{2,1,0:T(8,128)} copy(f32[1024,16,32]{0,2,1:T(8,128)S(1)} %bitcast.51) | data formatting | bytes 4194304 | tf_op jit(solution)/shard_map/transpose | solution.py:45
  54.1 6.2 %reshape_reshape.3 = f32[128,8,1,512]{3,1,0,2:T(8,128)S(1)} reshape(f32[1024,16,32]{2,1,0:T(8,128)} %copy.11) | data formatting | bytes 4194304 | tf_op jit(solution)/shard_map/reshape;reshape | solution.py:67
  62.5 6.5 %all-to-all-start = ((f32[128,8,1,512]{0,1,2,3:T(8,128)}), f32[128,8,1,512]{0,1,2,3:T(8,128)S(1)}, u32[]{:S(2)}, u32[]{:S(2)}) async-start(f32[128,8,1,512]{0,1,2,3:T(8,128)} %copy.12), calls=%async_computation | async-start | bytes 4194304 | tf_op jit(solution)/shard_map/all_to_all | solution.py:68
  69.0 48.1 %all-to-all-done = f32[128,8,1,512]{0,1,2,3:T(8,128)S(1)} async-done(((f32[128,8,1,512]{0,1,2,3:T(8,128)}), f32[128,8,1,512]{0,1,2,3:T(8,128)S(1)}, u32[]{:S(2)}, u32[]{:S(2)}) %all-to-all-start) | async-done | bytes 2097184 | tf_op jit(solution)/shard_map/all_to_all | solution.py:68
  117.3 4.8 %copy.15 = f32[128,8,128]{1,0,2:T(8,128)} copy(f32[128,8,128]{0,1,2:T(8,128)S(1)} %reduce_max.27) | data formatting | bytes 1048576
  122.2 6.2 %select_reduce_fusion.1 = f32[128,128]{0,1:T(8,128)} fusion(f32[128,8,128]{1,0,2:T(8,128)} %copy.15, pred[128,8]{1,0:T(8,128)(4,1)S(1)} %broadcast_compare_fusion.1), kind=kLoop, calls=%fused_computation.17 | loop fusion | flops 245760 | bytes 590848 | tf_op jit(solution)/shard_map/reduce_sum | solution.py:69
  128.4 41.1 %all-reduce.2.cloned.1.call-done = f32[128,128]{0,1:T(8,128)} async-done(((f32[128,128]{0,1:T(8,128)}), f32[128,128]{0,1:T(8,128)}) %all-reduce.2.cloned.1.call-update) | async-done | bytes 65552 | tf_op jit(solution)/shard_map/psum | solution.py:70
  171.3 15.1 %all-gather.3 = f32[8,1,128]{2,1,0:T(1,128)S(1)} all-gather(f32[1,1,128]{2,1,0:T(1,128)S(1)} %bitcast.55), channel_id=3, replica_groups=mesh['gx'=2,'gy'=4,'gz'=4] {'gx','gz'}, dimensions={0}, use_global_device_ids=true | all-gather | bytes 4608 | tf_op jit(solution)/shard_map/all_gather | solution.py:12
  186.3 12.8 %all-gather.2 = f32[8,1,128]{2,1,0:T(1,128)S(1)} all-gather(f32[1,1,128]{2,1,0:T(1,128)S(1)} %bitcast.54), channel_id=2, replica_groups=mesh['gx'=2,'gy'=4,'gz'=4] {'gx','gz'}, dimensions={0}, use_global_device_ids=true | all-gather | bytes 4608 | tf_op jit(solution)/shard_map/all_gather | solution.py:12
  (91 shorter events, 13.4 us)
Async XLA Ops:
  62.5 6.5 %copy-start = (s32[128]{0:T(128)S(1)}, s32[128]{0:T(128)}, u32[]{:S(2)}) copy-start(s32[128]{0:T(128)} %param.11) | copy-start | bytes 1540
  62.5 54.7 %all-to-all-start = ((f32[128,8,1,512]{0,1,2,3:T(8,128)}), f32[128,8,1,512]{0,1,2,3:T(8,128)S(1)}, u32[]{:S(2)}, u32[]{:S(2)}) async-start(f32[128,8,1,512]{0,1,2,3:T(8,128)} %copy.12), calls=%async_computation | async-start | bytes 4194304 | tf_op jit(solution)/shard_map/all_to_all | solution.py:68
  68.9 100.6 %all-reduce.2.cloned.1.call-start = ((), (), s32[]{:S(2)}) async-start(), calls=%async_computation.1 | async-start | bytes 131072 | tf_op jit(solution)/shard_map/psum | solution.py:70
Sparse Core Ops, SparseCore 0:
  128.5 40.9 all-reduce.1
where the time goes:
time: 209 us; the launch traced here: 208 us
  waiting for transfers between devices  89.2 us (43%)
  matrix products  38.2 us (18%)
  blocking collectives  27.8 us (13%)
  local copies, waits for them, and re-layouts  21.3 us (10%)
  between operations  13.4 us (6%)
  other arithmetic  10.6 us (5%)
  starting transfers between devices  6.48 us (3%)
    all_to_all x1, waiting for transfers between devices, shards(): lax.all_to_all(spread, 'gz', split_axis=3, concat_axis=2, tiled=True)  48.1 us
    psum x1, waiting for transfers between devices, shards(): scores_here = lax.psum(partial_value, 'gy')  41.1 us
    dot_general x16, matrix products, block_maxima(): lax.dot_general(flat_queries, passage_tile, (((1,), (1,)), ((), ())), pre...  38.2 us
    all_gather x2, blocking collectives, combined_all(): everything = jax.tree.map(lambda part: lax.all_gather(part, axis), array)  27.8 us
    another operation x2, local copies, waits for them, and re-layouts, shards(): spread = maxima.reshape(query_count, query_rows, 1, passage_count)  8.32 us
    all_to_all x1, starting transfers between devices, shards(): lax.all_to_all(spread, 'gz', split_axis=3, concat_axis=2, tiled=True)  6.48 us
    reduce_sum x1, other arithmetic, shards(): partial_value = jnp.sum(jnp.where(counted, merged, 0.0), axis=1)  6.25 us
    transpose x1, local copies, waits for them, and re-layouts, token_maxima(): jnp.transpose(pieces, (1, 0, 2))  6.23 us
  transfers between devices with their start and end apart: 2, of which 2 were waited for; matrix products, arithmetic and copies ran while one was open for 0% of the time, Pallas kernels for 0%

commit v1 on v0

v1 whole, which is shorter than its diff:
```python
import functools

import jax
import jax.numpy as jnp
from jax import lax
from jax.experimental import pallas as pl
from jax.experimental.pallas import tpu as pltpu
from jax.sharding import PartitionSpec as P

masked_low = -1e30
MESH = pl.DeviceIdType.MESH
HOP_LAG = 3
PEER_LAG = 3
PER_CHUNK = 16


def kernel(
    sizes,
    queries,
    lengths,
    query_len,
    passages,
    out,
    x,
    masked_x,
    wide_queries,
    query_columns,
    limits,
    own_low,
    own_high,
    got_low,
    got_high,
    partials,
    forward,
    total,
    stats,
    load_sem,
    z_send,
    low_recv,
    high_recv,
    peer_send,
    peer_recv,
    forward_send,
    forward_recv,
    stat_send,
    stat_recv,
):
    nx, ny, nz = sizes
    gx, gy, gz = (lax.axis_index(name) for name in ("gx", "gy", "gz"))
    passage_count, token_count, width = x.shape
    query_count, query_rows, _ = queries.shape
    chunks, per_chunk, row_count = own_low.shape
    half_blocks = nz // 2
    per_block = chunks // half_blocks
    block_rows = passage_count // nz
    group = nx * nz
    me = gx * nz + gz

    def low_start(c):
        return (half_blocks - 1 - c // per_block) * block_rows + (c % per_block) * per_chunk

    def high_start(c):
        return half_blocks * block_rows + c * per_chunk

    def member(turn):
        index = lax.rem(me + turn, group)
        return index, (index // nz, gy, lax.rem(index, nz))

    barrier = pltpu.get_barrier_semaphore()
    for turn in range(1, ny):
        pl.semaphore_signal(
            barrier, inc=1, device_id={"gy": lax.rem(gy + turn, ny)}, device_id_type=MESH
        )

    def greet(turn, carry):
        pl.semaphore_signal(barrier, inc=1, device_id=member(turn)[1], device_id_type=MESH)
        return carry

    lax.fori_loop(1, group, greet, 0)

    def load(start, index):
        rows = pl.ds(start, per_chunk)
        return pltpu.make_async_copy(passages.at[rows], x.at[rows], load_sem.at[index])

    def start_loads(c, carry):
        load(low_start(c), c).start()
        load(high_start(c), chunks + c).start()
        return carry

    lax.fori_loop(0, chunks, start_loads, 0)

    wide_queries[...] = queries[...].astype(jnp.float32).reshape(row_count, width)
    for i in range(query_rows):
        tile = wide_queries[pl.ds(i, query_count, stride=query_rows), :]
        query_columns[:, i * query_count : (i + 1) * query_count] = tile.T.astype(jnp.bfloat16)

    first_token = (gz * token_count).astype(jnp.float32)
    for b in range(passage_count // 128):
        row = lengths[b : b + 1, :].astype(jnp.float32) - first_token
        limits[b * 128 : (b + 1) * 128, :] = jnp.broadcast_to(row, (128, 128)).T

    pl.semaphore_wait(barrier, ny - 1 + group - 1)

    token_ids = lax.broadcasted_iota(jnp.int32, (token_count, width), 0).astype(jnp.float32)
    tile_columns = 256

    def compute(own, c, start, index):
        load(start, index).wait()
        for p in range(per_chunk):
            tokens = x[start + p].astype(jnp.float32)
            usable = token_ids < limits[pl.ds(start + p, 1), :]
            tokens = jnp.where(usable, tokens, tokens[0:1, :])
            masked_x[p * token_count : (p + 1) * token_count, :] = tokens.astype(jnp.bfloat16)
        limit = limits[pl.ds(start, per_chunk), :]
        any_used = jnp.concatenate([limit] * (tile_columns // 128), axis=1) > 0.0
        for t in range(row_count // tile_columns):
            columns = slice(t * tile_columns, (t + 1) * tile_columns)
            scores = jnp.dot(
                masked_x[...], query_columns[:, columns], preferred_element_type=jnp.float32
            )
            best = jnp.max(scores.reshape(per_chunk, token_count, tile_columns), axis=1)
            own[c, :, columns] = jnp.where(any_used, best, masked_low)

    def z_copy(own, got, recv, send_index, c, target):
        return pltpu.make_async_remote_copy(
            src_ref=own.at[c],
            dst_ref=got.at[c],
            send_sem=z_send.at[send_index],
            recv_sem=recv.at[c],
            device_id={"gz": target},
            device_id_type=MESH,
        )

    def peer_copy(turn, slot, block, where):
        return pltpu.make_async_remote_copy(
            src_ref=partials.at[slot, where],
            dst_ref=partials.at[slot, where],
            send_sem=peer_send.at[turn],
            recv_sem=peer_recv.at[slot, block],
            device_id={"gy": lax.rem(gy + turn, ny)},
            device_id_type=MESH,
        )

    def finalise(own, c):
        counted = query_len[...] - gy * query_rows
        so_far = jnp.zeros((per_chunk, query_count), jnp.float32)
        for i in range(query_rows):
            values = own[c, :, i * query_count : (i + 1) * query_count]
            so_far = so_far + jnp.where(counted > i, values, 0.0)
        partials[gy, c] = so_far
        for turn in range(1, ny):
            peer_copy(turn, gy, c // per_block, c).start()

    def block_total(block):
        where = pl.ds(block * per_block, per_block)
        for turn in range(1, ny):
            slot = lax.rem(gy + turn, ny)
            peer_copy(turn, slot, block, where).wait_recv()
        summed = partials[0, where]
        for slot in range(1, ny):
            summed = summed + partials[slot, where]
        return summed.reshape(block_rows, query_count)

    def forward_copy(block):
        target = jnp.where(gz == 0, half_blocks - 1 - block, half_blocks + block)
        return pltpu.make_async_remote_copy(
            src_ref=forward.at[block],
            dst_ref=total,
            send_sem=forward_send.at[block],
            recv_sem=forward_recv,
            device_id={"gz": target},
            device_id_type=MESH,
        )

    at_end = (gz == 0) | (gz == nz - 1)

    def step(s, carry):
        @pl.when(s < chunks)
        def _():
            compute(own_low, s, low_start(s), s)
            compute(own_high, s, high_start(s), chunks + s)

        def travel(own, got, recv, send_index, c, is_first, is_last, target):
            @pl.when((c >= 0) & (c < chunks))
            def _():
                @pl.when(jnp.logical_not(is_first))
                def _():
                    z_copy(own, got, recv, send_index, c, target).wait_recv()
                    own[c] = jnp.maximum(own[c], got[c])

                @pl.when(jnp.logical_not(is_last))
                def _():
                    z_copy(own, got, recv, send_index, c, target).start()

                @pl.when(is_last)
                def _():
                    finalise(own, c)

        first, last = gz == 0, gz == nz - 1
        down = lax.rem(gz + nz - 1, nz)
        up = lax.rem(gz + 1, nz)
        travel(own_low, got_low, low_recv, 0, s - HOP_LAG * (nz - 1 - gz), last, first, down)
        travel(own_high, got_high, high_recv, 1, s - HOP_LAG * gz, first, last, up)

        ready = s - HOP_LAG * (nz - 1) - PEER_LAG
        for block in range(half_blocks - 1):
            @pl.when(at_end & (ready == (block + 1) * per_block - 1))
            def _():
                forward[block] = block_total(block)
                forward_copy(block).start()

        return carry

    lax.fori_loop(0, chunks + HOP_LAG * (nz - 1), step, 0)

    @pl.when(at_end)
    def _():
        total[...] = block_total(half_blocks - 1)

    @pl.when(jnp.logical_not(at_end))
    def _():
        forward_copy(0).wait_recv()

    scores = total[...]
    top = jnp.max(scores, axis=0, keepdims=True)
    summed = jnp.sum(jnp.exp(scores - top), axis=0, keepdims=True)
    row_ids = lax.broadcasted_iota(jnp.int32, stats.shape[1:], 0)
    stats[me] = jnp.where(row_ids == 0, top, summed)

    def stat_copy(slot, turn):
        return pltpu.make_async_remote_copy(
            src_ref=stats.at[slot],
            dst_ref=stats.at[slot],
            send_sem=stat_send.at[turn],
            recv_sem=stat_recv.at[slot],
            device_id=member(turn)[1],
            device_id_type=MESH,
        )

    def send_stats(turn, carry):
        stat_copy(me, turn).start()
        return carry

    lax.fori_loop(1, group, send_stats, 0)

    def wait_stats(turn, carry):
        stat_copy(member(turn)[0], turn).wait_recv()
        return carry

    lax.fori_loop(1, group, wait_stats, 0)
    tops = stats[:, 0, :]
    highest = jnp.max(tops, axis=0, keepdims=True)
    everything = jnp.sum(stats[:, 1, :] * jnp.exp(tops - highest), axis=0, keepdims=True)
    out[...] = (scores - (highest + jnp.log(everything))).T

    @pl.when(gz > 0)
    def _():
        whole = pl.ds(0, chunks)
        z_copy(own_low, got_low, low_recv, 0, whole, 0).wait_send()

    @pl.when(gz < nz - 1)
    def _():
        whole = pl.ds(0, chunks)
        z_copy(own_high, got_high, high_recv, 1, whole, 0).wait_send()

    @pl.when(at_end)
    def _():
        for turn in range(1, ny):
            peer_copy(turn, gy, 0, pl.ds(0, chunks)).wait_send()
        for block in range(half_blocks - 1):
            forward_copy(block).wait_send()

    def drain_stats(turn, carry):
        stat_copy(me, turn).wait_send()
        return carry

    lax.fori_loop(1, group, drain_stats, 0)


def shards(sizes, queries, passages, passage_len, query_len):
    nx, ny, nz = sizes
    query_count, query_rows, width = queries.shape
    passage_count, token_count, _ = passages.shape
    row_count = query_count * query_rows
    block_rows = passage_count // nz
    per_chunk = PER_CHUNK
    chunks = passage_count // 2 // per_chunk
    half_blocks = nz // 2
    maxima = pltpu.VMEM((chunks, per_chunk, row_count), jnp.float32)
    dma = pltpu.SemaphoreType.DMA
    vmem = pl.BlockSpec(memory_space=pltpu.VMEM)
    return pl.pallas_call(
        functools.partial(kernel, sizes),
        out_shape=jax.ShapeDtypeStruct((query_count, block_rows), jnp.float32),
        in_specs=[vmem, vmem, vmem, pl.BlockSpec(memory_space=pl.ANY)],
        out_specs=vmem,
        scratch_shapes=[
            pltpu.VMEM(passages.shape, passages.dtype),
            pltpu.VMEM((per_chunk * token_count, width), jnp.bfloat16),
            pltpu.VMEM((row_count, width), jnp.float32),
            pltpu.VMEM((width, row_count), jnp.bfloat16),
            pltpu.VMEM((passage_count, 128), jnp.float32),
            maxima,
            maxima,
            maxima,
            maxima,
            pltpu.VMEM((ny, chunks, per_chunk, query_count), jnp.float32),
            pltpu.VMEM((max(1, half_blocks - 1), block_rows, query_count), jnp.float32),
            pltpu.VMEM((block_rows, query_count), jnp.float32),
            pltpu.VMEM((nx * nz, 8, query_count), jnp.float32),
            dma((2 * chunks,)),
            dma((2,)),
            dma((chunks,)),
            dma((chunks,)),
            dma((ny,)),
            dma((ny, half_blocks)),
            dma((max(1, half_blocks - 1),)),
            dma,
            dma((nx * nz,)),
            dma((nx * nz,)),
        ],
        compiler_params=pltpu.CompilerParams(
            collective_id=0, has_side_effects=True, vmem_limit_bytes=48 * 1024 * 1024
        ),
    )(
        queries,
        passage_len.reshape(passage_count // 128, 128),
        query_len.reshape(1, query_count),
        passages,
    )


def solution(mesh):
    sizes = tuple(mesh.shape[name] for name in ("gx", "gy", "gz"))
    return jax.shard_map(
        functools.partial(shards, sizes),
        mesh=mesh,
        in_specs=(P(None, "gy", None), P("gx", "gz", None), P("gx"), P()),
        out_specs=P(None, ("gx", "gz")),
        check_vma=False,
    )
```

time: 209 us -> 51.9 us (0.25)
  waiting for transfers between devices: 89.2 us -> 0 us
  Pallas kernels: 0 us -> 48.8 us
  matrix products: 38.2 us -> 0 us
  blocking collectives: 27.8 us -> 0 us
  local copies, waits for them, and re-layouts: 21.3 us -> 2.92 us
  between operations: 13.4 us -> 0.01 us
  other arithmetic: 10.6 us -> 0 us
  starting transfers between devices: 6.48 us -> 0 us
    pallas_call x0 -> x1, Pallas kernels: none -> 48.8 us  [shards(): pl.pallas_call(functools.partial(kernel, sizes), out_shape=jax.ShapeDtype...]
    all_to_all x1 -> x0, waiting for transfers between devices: 48.1 us -> none  [shards(): lax.all_to_all(spread, 'gz', split_axis=3, concat_axis=2, tiled=True)]
    psum x1 -> x0, waiting for transfers between devices: 41.1 us -> none  [shards(): scores_here = lax.psum(partial_value, 'gy')]
    dot_general x16 -> x0, matrix products: 38.2 us -> none  [block_maxima(): lax.dot_general(flat_queries, passage_tile, (((1,), (1,)), ((), ())), pre...]
    all_gather x2 -> x0, blocking collectives: 27.8 us -> none  [combined_all(): everything = jax.tree.map(lambda part: lax.all_gather(part, axis), array)]
    another operation x2 -> x0, local copies, waits for them, and re-layouts: 8.32 us -> none  [shards(): spread = maxima.reshape(query_count, query_rows, 1, passage_count)]
    reduce_sum x2 -> x0, other arithmetic: 7.12 us -> none  [the longest x1 6.25 us: shards(): partial_value = jnp.sum(jnp.where(counted, merged, 0.0), axis=1)]
    all_to_all x1 -> x0, starting transfers between devices: 6.48 us -> none  [shards(): lax.all_to_all(spread, 'gz', split_axis=3, concat_axis=2, tiled=True)]
  transfers between devices with their start and end apart: 2 -> 0, of which waited for: 2 -> 0; matrix products, arithmetic and copies ran while one was open for 0% -> 0% of each run, Pallas kernels for 0% -> 0%
where the time goes in v1:
time: 51.9 us; the launch traced here: 51.7 us
  Pallas kernels  48.8 us (94%)
  local copies, waits for them, and re-layouts  2.92 us (6%)
    pallas_call x1, Pallas kernels, shards(): pl.pallas_call(functools.partial(kernel, sizes), out_shape=jax.ShapeDtype...  48.8 us
    unnamed x7, local copies, waits for them, and re-layouts  2.92 us

profile of v1, /device:TPU:0, one launch (start us, length us, event | category | flops | bytes accessed | tf_op | source)
XLA Modules:
  0.0 51.7 jit_solution(10904245324746233332)
XLA Ops:
  0.0 0.0 copy-start
  0.0 0.9 %copy-done = bf16[128,8,128]{2,1,0:T(8,128)(2,1)S(1)} copy-done((bf16[128,8,128]{2,1,0:T(8,128)(2,1)S(1)}, bf16[128,8,128]{2,1,0:T(8,128)(2,1)}, u32[]{:S(2)}) %copy-start) | copy-done | bytes 262168
  1.0 0.0 copy-start.1
  1.0 0.7 %copy-done.1 = s32[512]{0:T(512)S(1)} copy-done((s32[512]{0:T(512)S(1)}, s32[512]{0:T(512)}, u32[]{:S(2)}) %copy-start.1) | copy-done | bytes 2072
  1.6 0.0 copy-start.2
  1.6 0.7 %copy-done.2 = s32[128]{0:T(128)S(1)} copy-done((s32[128]{0:T(128)S(1)}, s32[128]{0:T(128)}, u32[]{:S(2)}) %copy-start.2) | copy-done | bytes 536
  2.3 48.8 %shard_map.46 = f32[128,128]{1,0:T(8,128)S(1)} custom-call(bf16[128,8,128]{2,1,0:T(8,128)(2,1)S(1)} %copy-done, s32[4,128]{1,0:T(4,128)S(1)} %bitcast.2, s32[1,128]{1,0:T(1,128)S(1)} %bitcast.3, bf16[512,64,128]{2,1,0:T(8,128)(2,1)} %passages.1), custom_call_target="tpu_custom_call" | custom-call | tf_op jit(solution)/shard_map/pallas_call | solution.py:292
  51.0 0.6 %copy.6 = f32[128,128]{1,0:T(8,128)} copy(f32[128,128]{1,0:T(8,128)S(1)} %shard_map.46) | data formatting | bytes 131072
Async XLA Ops:
  0.0 0.9 %copy-start = (bf16[128,8,128]{2,1,0:T(8,128)(2,1)S(1)}, bf16[128,8,128]{2,1,0:T(8,128)(2,1)}, u32[]{:S(2)}) copy-start(bf16[128,8,128]{2,1,0:T(8,128)(2,1)} %queries.1) | copy-start | bytes 786436
  1.0 0.7 %copy-start.1 = (s32[512]{0:T(512)S(1)}, s32[512]{0:T(512)}, u32[]{:S(2)}) copy-start(s32[512]{0:T(512)} %param.6) | copy-start | bytes 6148
  1.6 0.7 %copy-start.2 = (s32[128]{0:T(128)S(1)}, s32[128]{0:T(128)}, u32[]{:S(2)}) copy-start(s32[128]{0:T(128)} %param.7) | copy-start | bytes 1540

commit v2 on v1

--- a/solution.py
+++ b/solution.py
@@ -9,18 +9,22 @@
 
 masked_low = -1e30
 MESH = pl.DeviceIdType.MESH
-HOP_LAG = 3
+HOP_LAG = 4
 PEER_LAG = 3
 PER_CHUNK = 16
+PARTS = 2
 
 
 def kernel(
     sizes,
+    queries_in,
+    lengths_in,
+    query_len_in,
+    passages,
+    out,
     queries,
     lengths,
     query_len,
-    passages,
-    out,
     x,
     masked_x,
     wide_queries,
@@ -34,6 +38,7 @@
     forward,
     total,
     stats,
+    small_sem,
     load_sem,
     z_send,
     low_recv,
@@ -49,7 +54,9 @@
     gx, gy, gz = (lax.axis_index(name) for name in ("gx", "gy", "gz"))
     passage_count, token_count, width = x.shape
     query_count, query_rows, _ = queries.shape
-    chunks, per_chunk, row_count = own_low.shape
+    slots, per_chunk, row_count = own_low.shape
+    chunks = slots - 1
+    part_rows = per_chunk // PARTS
     half_blocks = nz // 2
     per_block = chunks // half_blocks
     block_rows = passage_count // nz
@@ -78,6 +85,15 @@
 
     lax.fori_loop(1, group, greet, 0)
 
+    small = [
+        pltpu.make_async_copy(source, target, small_sem.at[index])
+        for index, (source, target) in enumerate(
+            ((queries_in, queries), (lengths_in, lengths), (query_len_in, query_len))
+        )
+    ]
+    for copy in small:
+        copy.start()
+
     def load(start, index):
         rows = pl.ds(start, per_chunk)
         return pltpu.make_async_copy(passages.at[rows], x.at[rows], load_sem.at[index])
@@ -88,6 +104,9 @@
         return carry
 
     lax.fori_loop(0, chunks, start_loads, 0)
+
+    for copy in small:
+        copy.wait()
 
     wide_queries[...] = queries[...].astype(jnp.float32).reshape(row_count, width)
     for i in range(query_rows):
@@ -99,63 +118,92 @@
         row = lengths[b : b + 1, :].astype(jnp.float32) - first_token
         limits[b * 128 : (b + 1) * 128, :] = jnp.broadcast_to(row, (128, 128)).T
 
-    pl.semaphore_wait(barrier, ny - 1 + group - 1)
-
     token_ids = lax.broadcasted_iota(jnp.int32, (token_count, width), 0).astype(jnp.float32)
     tile_columns = 256
 
-    def compute(own, c, start, index):
-        load(start, index).wait()
-        for p in range(per_chunk):
-            tokens = x[start + p].astype(jnp.float32)
-            usable = token_ids < limits[pl.ds(start + p, 1), :]
-            tokens = jnp.where(usable, tokens, tokens[0:1, :])
-            masked_x[p * token_count : (p + 1) * token_count, :] = tokens.astype(jnp.bfloat16)
-        limit = limits[pl.ds(start, per_chunk), :]
+    def compute(c):
+        starts = (low_start(c), high_start(c))
+        limit = []
+        for half, start in enumerate(starts):
+            for p in range(per_chunk):
+                tokens = x[start + p].astype(jnp.float32)
+                usable = token_ids < limits[pl.ds(start + p, 1), :]
+                tokens = jnp.where(usable, tokens, tokens[0:1, :])
+                row = (half * per_chunk + p) * token_count
+                masked_x[row : row + token_count, :] = tokens.astype(jnp.bfloat16)
+            limit.append(limits[pl.ds(start, per_chunk), :])
+        limit = jnp.concatenate(limit, axis=0)
         any_used = jnp.concatenate([limit] * (tile_columns // 128), axis=1) > 0.0
         for t in range(row_count // tile_columns):
             columns = slice(t * tile_columns, (t + 1) * tile_columns)
             scores = jnp.dot(
                 masked_x[...], query_columns[:, columns], preferred_element_type=jnp.float32
             )
-            best = jnp.max(scores.reshape(per_chunk, token_count, tile_columns), axis=1)
-            own[c, :, columns] = jnp.where(any_used, best, masked_low)
-
-    def z_copy(own, got, recv, send_index, c, target):
-        return pltpu.make_async_remote_copy(
-            src_ref=own.at[c],
-            dst_ref=got.at[c],
-            send_sem=z_send.at[send_index],
-            recv_sem=recv.at[c],
-            device_id={"gz": target},
-            device_id_type=MESH,
-        )
+            best = jnp.max(scores.reshape(2 * per_chunk, token_count, tile_columns), axis=1)
+            best = jnp.where(any_used, best, masked_low)
+            own_low[c, :, columns] = best[:per_chunk]
+            own_high[c, :, columns] = best[per_chunk:]
+
+    class Flow:
+        def __init__(self, own, got, recv, send_index, hops, is_last, target):
+            self.own, self.got, self.recv, self.send_index = own, got, recv, send_index
+            self.is_first, self.is_last, self.target = hops == 0, is_last, target
+            self.lag = HOP_LAG * hops
+
+        def copy(self, source, c, part):
+            rows = pl.ds(part * part_rows, part_rows)
+            return pltpu.make_async_remote_copy(
+                src_ref=source.at[c, rows],
+                dst_ref=self.got.at[c, rows],
+                send_sem=z_send.at[self.send_index],
+                recv_sem=self.recv.at[c, part],
+                device_id={"gz": self.target},
+                device_id_type=MESH,
+            )
+
+        def merge(self, c, rows):
+            self.got[c, rows] = jnp.maximum(self.got[c, rows], self.own[c, rows])
+
+        def pass_on(self, c, part):
+            @pl.when(jnp.logical_not(self.is_last))
+            def _():
+                self.copy(self.got, c, part).start()
+
+            @pl.when(self.is_last)
+            def _():
+                finalise(self.got, c, part)
+
+    first, last = gz == 0, gz == nz - 1
+    low = Flow(own_low, got_low, low_recv, 0, nz - 1 - gz, first, lax.rem(gz + nz - 1, nz))
+    high = Flow(own_high, got_high, high_recv, 1, gz, last, lax.rem(gz + 1, nz))
+    flows = (low, high)
 
     def peer_copy(turn, slot, block, where):
         return pltpu.make_async_remote_copy(
-            src_ref=partials.at[slot, where],
-            dst_ref=partials.at[slot, where],
+            src_ref=partials.at[(slot, *where)],
+            dst_ref=partials.at[(slot, *where)],
             send_sem=peer_send.at[turn],
             recv_sem=peer_recv.at[slot, block],
             device_id={"gy": lax.rem(gy + turn, ny)},
             device_id_type=MESH,
         )
 
-    def finalise(own, c):
+    def finalise(merged, c, part):
+        rows = pl.ds(part * part_rows, part_rows)
         counted = query_len[...] - gy * query_rows
-        so_far = jnp.zeros((per_chunk, query_count), jnp.float32)
+        so_far = jnp.zeros((part_rows, query_count), jnp.float32)
         for i in range(query_rows):
-            values = own[c, :, i * query_count : (i + 1) * query_count]
+            values = merged[c, rows, i * query_count : (i + 1) * query_count]
             so_far = so_far + jnp.where(counted > i, values, 0.0)
-        partials[gy, c] = so_far
+        partials[gy, c, rows] = so_far
         for turn in range(1, ny):
-            peer_copy(turn, gy, c // per_block, c).start()
+            peer_copy(turn, gy, c // per_block, (c, rows)).start()
 
     def block_total(block):
         where = pl.ds(block * per_block, per_block)
         for turn in range(1, ny):
             slot = lax.rem(gy + turn, ny)
-            peer_copy(turn, slot, block, where).wait_recv()
+            peer_copy(turn, slot, block, (where,)).wait_recv()
         summed = partials[0, where]
         for slot in range(1, ny):
             summed = summed + partials[slot, where]
@@ -174,34 +222,7 @@
 
     at_end = (gz == 0) | (gz == nz - 1)
 
-    def step(s, carry):
-        @pl.when(s < chunks)
-        def _():
-            compute(own_low, s, low_start(s), s)
-            compute(own_high, s, high_start(s), chunks + s)
-
-        def travel(own, got, recv, send_index, c, is_first, is_last, target):
-            @pl.when((c >= 0) & (c < chunks))
-            def _():
-                @pl.when(jnp.logical_not(is_first))
-                def _():
-                    z_copy(own, got, recv, send_index, c, target).wait_recv()
-                    own[c] = jnp.maximum(own[c], got[c])
-
-                @pl.when(jnp.logical_not(is_last))
-                def _():
-                    z_copy(own, got, recv, send_index, c, target).start()
-
-                @pl.when(is_last)
-                def _():
-                    finalise(own, c)
-
-        first, last = gz == 0, gz == nz - 1
-        down = lax.rem(gz + nz - 1, nz)
-        up = lax.rem(gz + 1, nz)
-        travel(own_low, got_low, low_recv, 0, s - HOP_LAG * (nz - 1 - gz), last, first, down)
-        travel(own_high, got_high, high_recv, 1, s - HOP_LAG * gz, first, last, up)
-
+    def forward_ready_block(s):
         ready = s - HOP_LAG * (nz - 1) - PEER_LAG
         for block in range(half_blocks - 1):
             @pl.when(at_end & (ready == (block + 1) * per_block - 1))
@@ -209,9 +230,59 @@
                 forward[block] = block_total(block)
                 forward_copy(block).start()
 
-        return carry
-
-    lax.fori_loop(0, chunks + HOP_LAG * (nz - 1), step, 0)
+    def step(s, carry):
+        load(low_start(s), s).wait()
+        load(high_start(s), chunks + s).wait()
+        waiting = []
+        for flow in flows:
+            c = s - flow.lag
+            merging = jnp.logical_not(flow.is_first) & (c >= 0)
+            waiting.append((flow, c, merging))
+
+            @pl.when(merging)
+            def _():
+                for part in range(PARTS):
+                    flow.copy(flow.got, c, part).wait_recv()
+
+        for flow, c, merging in waiting:
+            flow.merge(jnp.where(merging, c, chunks), pl.ds(0, per_chunk))
+        compute(s)
+
+        @pl.when(s == 0)
+        def _():
+            pl.semaphore_wait(barrier, ny - 1 + group - 1)
+
+        for flow, c, merging in waiting:
+            @pl.when(merging)
+            def _():
+                for part in range(PARTS):
+                    flow.pass_on(c, part)
+
+            @pl.when(flow.is_first)
+            def _():
+                for part in range(PARTS):
+                    flow.copy(flow.own, s, part).start()
+
+        forward_ready_block(s)
+        return carry
+
+    lax.fori_loop(0, chunks, step, 0)
+
+    def drain(s, carry):
+        for flow in flows:
+            c = s - flow.lag
+
+            @pl.when(jnp.logical_not(flow.is_first) & (c >= 0) & (c < chunks))
+            def _():
+                for part in range(PARTS):
+                    flow.copy(flow.got, c, part).wait_recv()
+                    flow.merge(c, pl.ds(part * part_rows, part_rows))
+                    flow.pass_on(c, part)
+
+        forward_ready_block(s)
+        return carry
+
+    lax.fori_loop(chunks, chunks + HOP_LAG * (nz - 1), drain, 0)
 
     @pl.when(at_end)
     def _():
@@ -253,20 +324,23 @@
     everything = jnp.sum(stats[:, 1, :] * jnp.exp(tops - highest), axis=0, keepdims=True)
     out[...] = (scores - (highest + jnp.log(everything))).T
 
-    @pl.when(gz > 0)
-    def _():
-        whole = pl.ds(0, chunks)
-        z_copy(own_low, got_low, low_recv, 0, whole, 0).wait_send()
-
-    @pl.when(gz < nz - 1)
-    def _():
-        whole = pl.ds(0, chunks)
-        z_copy(own_high, got_high, high_recv, 1, whole, 0).wait_send()
+    for flow in flows:
+        @pl.when(jnp.logical_not(flow.is_last))
+        def _():
+            whole = pl.ds(0, chunks)
+            pltpu.make_async_remote_copy(
+                src_ref=flow.got.at[whole],
+                dst_ref=flow.got.at[whole],
+                send_sem=z_send.at[flow.send_index],
+                recv_sem=flow.recv.at[0, 0],
+                device_id={"gz": flow.target},
+                device_id_type=MESH,
+            ).wait_send()
 
     @pl.when(at_end)
     def _():
         for turn in range(1, ny):
-            peer_copy(turn, gy, 0, pl.ds(0, chunks)).wait_send()
+            peer_copy(turn, gy, 0, (pl.ds(0, chunks),)).wait_send()
         for block in range(half_blocks - 1):
             forward_copy(block).wait_send()
 
@@ -286,17 +360,20 @@
     per_chunk = PER_CHUNK
     chunks = passage_count // 2 // per_chunk
     half_blocks = nz // 2
-    maxima = pltpu.VMEM((chunks, per_chunk, row_count), jnp.float32)
+    maxima = pltpu.VMEM((chunks + 1, per_chunk, row_count), jnp.float32)
     dma = pltpu.SemaphoreType.DMA
-    vmem = pl.BlockSpec(memory_space=pltpu.VMEM)
+    anywhere = pl.BlockSpec(memory_space=pltpu.HBM)
     return pl.pallas_call(
         functools.partial(kernel, sizes),
         out_shape=jax.ShapeDtypeStruct((query_count, block_rows), jnp.float32),
-        in_specs=[vmem, vmem, vmem, pl.BlockSpec(memory_space=pl.ANY)],
-        out_specs=vmem,
+        in_specs=[anywhere] * 4,
+        out_specs=pl.BlockSpec(memory_space=pltpu.VMEM),
         scratch_shapes=[
+            pltpu.VMEM(queries.shape, queries.dtype),
+            pltpu.VMEM((passage_count // 128, 128), passage_len.dtype),
+            pltpu.VMEM((1, query_count), query_len.dtype),
             pltpu.VMEM(passages.shape, passages.dtype),
-            pltpu.VMEM((per_chunk * token_count, width), jnp.bfloat16),
+            pltpu.VMEM((2 * per_chunk * token_count, width), jnp.bfloat16),
             pltpu.VMEM((row_count, width), jnp.float32),
             pltpu.VMEM((width, row_count), jnp.bfloat16),
             pltpu.VMEM((passage_count, 128), jnp.float32),
@@ -308,10 +385,11 @@
             pltpu.VMEM((max(1, half_blocks - 1), block_rows, query_count), jnp.float32),
             pltpu.VMEM((block_rows, query_count), jnp.float32),
             pltpu.VMEM((nx * nz, 8, query_count), jnp.float32),
+            dma((3,)),
             dma((2 * chunks,)),
             dma((2,)),
-            dma((chunks,)),
-            dma((chunks,)),
+            dma((chunks, PARTS)),
+            dma((chunks, PARTS)),
             dma((ny,)),
             dma((ny, half_blocks)),
             dma((max(1, half_blocks - 1),)),

time: 51.9 us -> 52.9 us (1.019)
  Pallas kernels: 48.8 us -> 49.8 us
    pallas_call x1, Pallas kernels: 48.8 us -> 49.8 us  [shards(): pl.pallas_call(functools.partial(kernel, sizes), out_shape=jax.ShapeDtype...]
where the time goes in v2:
time: 52.9 us; the launch traced here: 52.7 us
  Pallas kernels  49.8 us (94%)
  local copies, waits for them, and re-layouts  2.92 us (6%)
    pallas_call x1, Pallas kernels, shards(): pl.pallas_call(functools.partial(kernel, sizes), out_shape=jax.ShapeDtype...  49.8 us
    unnamed x7, local copies, waits for them, and re-layouts  2.92 us

profile of v2, /device:TPU:0, one launch (start us, length us, event | category | flops | bytes accessed | tf_op | source)
XLA Modules:
  0.0 52.7 jit_solution(6743349950518233182)
XLA Ops:
  0.0 0.0 copy-start
  0.0 0.9 %copy-done = bf16[128,8,128]{2,1,0:T(8,128)(2,1)S(1)} copy-done((bf16[128,8,128]{2,1,0:T(8,128)(2,1)S(1)}, bf16[128,8,128]{2,1,0:T(8,128)(2,1)}, u32[]{:S(2)}) %copy-start) | copy-done | bytes 262168
  1.0 0.0 copy-start.1
  1.0 0.7 %copy-done.1 = s32[512]{0:T(512)S(1)} copy-done((s32[512]{0:T(512)S(1)}, s32[512]{0:T(512)}, u32[]{:S(2)}) %copy-start.1) | copy-done | bytes 2072
  1.6 0.0 copy-start.2
  1.6 0.7 %copy-done.2 = s32[128]{0:T(128)S(1)} copy-done((s32[128]{0:T(128)S(1)}, s32[128]{0:T(128)}, u32[]{:S(2)}) %copy-start.2) | copy-done | bytes 536
  2.3 49.8 %shard_map.46 = f32[128,128]{1,0:T(8,128)S(1)} custom-call(bf16[128,8,128]{2,1,0:T(8,128)(2,1)S(1)} %copy-done, s32[4,128]{1,0:T(4,128)S(1)} %bitcast.2, s32[1,128]{1,0:T(1,128)S(1)} %bitcast.3, bf16[512,64,128]{2,1,0:T(8,128)(2,1)} %passages.1), custom_call_target="tpu_custom_call" | custom-call | tf_op jit(solution)/shard_map/pallas_call | solution.py:366
  52.1 0.6 %copy.6 = f32[128,128]{1,0:T(8,128)} copy(f32[128,128]{1,0:T(8,128)S(1)} %shard_map.46) | data formatting | bytes 131072
Async XLA Ops:
  0.0 0.9 %copy-start = (bf16[128,8,128]{2,1,0:T(8,128)(2,1)S(1)}, bf16[128,8,128]{2,1,0:T(8,128)(2,1)}, u32[]{:S(2)}) copy-start(bf16[128,8,128]{2,1,0:T(8,128)(2,1)} %queries_in.1) | copy-start | bytes 786436
  1.0 0.7 %copy-start.1 = (s32[512]{0:T(512)S(1)}, s32[512]{0:T(512)}, u32[]{:S(2)}) copy-start(s32[512]{0:T(512)} %param.6) | copy-start | bytes 6148
  1.6 0.7 %copy-start.2 = (s32[128]{0:T(128)S(1)}, s32[128]{0:T(128)}, u32[]{:S(2)}) copy-start(s32[128]{0:T(128)} %param.7) | copy-start | bytes 1540
